TPU v7x, 32 devices: a whole 2x2x4 slice. The times are simulated.
32 devices in a mesh: patch: 16 (over z, y, x), batch: 2 (over core).
Axes of the slice: x: 2, y: 2, z: 4, core: 2. Of those that a mesh axis runs over, the one named last changes fastest.
Arguments:
- tokens: bfloat16 [4096, 1152], P(('batch', 'patch')), parts along dimension 0, may hold values from -6 to 6
- slots: int32 [4096], P(('batch', 'patch')), parts along dimension 0, may hold values from 0 to 127, as said below
- counts: int32 [32], P(('batch', 'patch')), parts along dimension 0, may hold values from 32 to 128, as said below
- shift: float32 [1152], replicated, may hold values from -3 to 3
- scale: float32 [1152], replicated, may hold values from -3 to 3
- gate: float32 [1152], replicated, may hold values from -4 to 4
- w_qkv: bfloat16 [1152, 3456], replicated, may hold values from -1 to 1
- w_out: bfloat16 [1152, 1152], replicated, may hold values from -0.1875 to 0.1875
Outputs:
- result: bfloat16 [4096, 1152], P(('batch', 'patch')), parts along dimension 0
There are 2 independent parts, one for each index of `batch`. A program takes and returns all parts, laid end to end along the dimension named above; an argument that names none is the same for every part. Nothing has to cross between parts.
Inputs may be any that keep to these rules, and one draw needn't show every extreme that they name: `counts`: at least a quarter of each block's slots are live. The live slots of all blocks of an image number exactly 80 times the number of patch devices, and all blocks of some device are full. `slots`: every token's slot is below its block's count, and every slot below the count holds at least one token.
All inputs are finite; a program needn't handle non-finite values.
Results may differ from a plain program's by a relative error of at most 0.011.
Values may be sent and summed in bfloat16 or wider, within the bound.
A program may use at most 192 MiB of HBM per device.

v0:
```python
import functools
import math

import jax
import jax.numpy as jnp
from jax import lax
from jax.experimental import pallas as pl
from jax.experimental.pallas import tpu as pltpu
from jax.sharding import PartitionSpec as P

HEADS = 16
BLK = 128
AUG = 8
CHUNK = 384
MESH = pl.DeviceIdType.MESH


def layer_norm(merged, shift, scale):
    values = merged.astype(jnp.float32)
    center = jnp.mean(values, axis=-1, keepdims=True)
    spread = jnp.mean((values - center) ** 2, axis=-1, keepdims=True)
    return ((values - center) * lax.rsqrt(spread + 1e-06) * (1.0 + scale) + shift).astype(
        jnp.bfloat16
    )


def merge(tokens, slots, counts):
    rows, width = tokens.shape
    nblk = rows // BLK
    onehot = slots.reshape(nblk, BLK)[:, :, None] == jnp.arange(BLK, dtype=jnp.int32)[None, None, :]
    sums = jnp.einsum(
        "bts,btd->bsd",
        onehot.astype(jnp.bfloat16),
        tokens.reshape(nblk, BLK, width),
        preferred_element_type=jnp.float32,
    )
    members = jnp.sum(onehot.astype(jnp.float32), axis=1)
    merged = (
        (sums / jnp.maximum(members, 1.0)[:, :, None]).astype(jnp.bfloat16).reshape(rows, width)
    )
    alive = (jnp.arange(BLK, dtype=jnp.int32)[None, :] < counts[:, None]).reshape(rows)
    bias = jnp.where(alive, jnp.log(jnp.maximum(members, 1.0)).reshape(rows), -1e30)
    return onehot, merged, bias


def attention(
    n, hd, slots, counts, tokens, shift, scale, w_hbm, out, w, turned, kq_msg, v_msg,
    kq_in, v_in, qs, ks, vs, probs, part, w_sem, *sems
):
    kq_out_sem, kq_in_sem, v_out_sem, v_in_sem, r_out_sem, r_in_sem = sems
    me = lax.axis_index("patch")
    rows, width = tokens.shape
    aug = hd + AUG

    def weights(p):
        return pltpu.make_async_copy(w_hbm.at[:, pl.ds(p * width, width)], w.at[p], w_sem.at[p])

    for p in (1, 0, 2):
        weights(p).start()
    barrier = pltpu.get_barrier_semaphore()
    for i in range(1, n):
        pl.semaphore_signal(
            barrier, inc=1, device_id={"patch": lax.rem(me + i, n)}, device_id_type=MESH
        )

    onehot = slots[...] == lax.broadcasted_iota(jnp.int32, (rows, rows), 0)
    exact = onehot.astype(jnp.float32)
    picks = exact.astype(jnp.bfloat16)
    sums = jnp.dot(picks, tokens[...], preferred_element_type=jnp.float32)
    members = jnp.sum(exact, axis=1, keepdims=True)
    merged = (sums / jnp.maximum(members, 1.0)).astype(jnp.bfloat16)
    normed = layer_norm(merged, shift[...][None], scale[...][None])
    sizes = lax.dot_general(
        jnp.ones((AUG, rows), jnp.bfloat16),
        picks,
        (((1,), (1,)), ((), ())),
        preferred_element_type=jnp.float32,
    )
    alive = lax.broadcasted_iota(jnp.int32, (AUG, rows), 1) < counts[...]
    lift = jnp.where(alive, jnp.log(jnp.maximum(sizes, 1.0)), -1e30) * math.sqrt(hd)
    high = lift.astype(jnp.bfloat16).astype(jnp.float32)
    rest = lift - high
    middle = rest.astype(jnp.bfloat16).astype(jnp.float32)
    low = rest - middle
    line = lax.broadcasted_iota(jnp.int32, (AUG, rows), 0)
    extra = jnp.where(
        line == 0, high, jnp.where(line == 1, middle, jnp.where(line == 2, low, 0.0))
    )

    def project(p):
        weights(p).wait()
        for at in range(0, width, CHUNK):
            piece = jnp.dot(normed, w[p, :, at : at + CHUNK], preferred_element_type=jnp.float32)
            turned[at : at + CHUNK] = piece.T

    def head(h):
        return turned[h * hd : (h + 1) * hd]

    project(1)
    for h in range(n):
        kq_msg[h, :aug] = jnp.concatenate([head(h), extra], axis=0).astype(jnp.bfloat16)
    project(0)
    for h in range(n):
        kq_msg[h, aug:] = head(h).astype(jnp.bfloat16)

    def copy(src_ref, dst_ref, send, recv, dst, src):
        return pltpu.make_async_remote_copy(
            src_ref=src_ref.at[dst],
            dst_ref=dst_ref.at[src],
            send_sem=send.at[dst],
            recv_sem=recv.at[src],
            device_id={"patch": dst},
            device_id_type=MESH,
        )

    def kq_to(dst, src):
        return copy(kq_msg, kq_in, kq_out_sem, kq_in_sem, dst, src)

    def v_to(dst, src):
        return copy(v_msg, v_in, v_out_sem, v_in_sem, dst, src)

    def result_to(dst, src):
        return copy(part, out, r_out_sem, r_in_sem, dst, src)

    pl.semaphore_wait(barrier, n - 1)
    for i in range(1, n):
        kq_to(lax.rem(me + i, n), me).start()
    project(2)
    for h in range(n):
        v_msg[h] = head(h).astype(jnp.bfloat16)
    for i in range(1, n):
        v_to(lax.rem(me + i, n), me).start()

    tail = jnp.ones((AUG, rows), jnp.bfloat16)

    def columns(src):
        return pl.ds(pl.multiple_of(src * rows, rows), rows)

    def place_kq(src, block):
        ks[:, columns(src)] = block[:aug]
        qs[:, columns(src)] = jnp.concatenate([block[aug:], tail], axis=0)

    def place_v(src, block):
        vs[:, columns(src)] = jnp.concatenate([block, tail], axis=0)

    place_kq(me, kq_msg[me])
    for i in range(1, n):
        src = lax.rem(me + n - i, n)
        kq_to(src, src).wait_recv()
        place_kq(src, kq_in[src])

    factor = math.log2(math.e) / math.sqrt(hd)
    wide = 2 * rows
    pairs = n // 2

    def pair_of(c):
        return lax.rem(me // 2 + c, pairs)

    def send_pair(c):
        for t in range(2):
            dst = 2 * pair_of(c) + t

            @pl.when(dst != me)
            def _():
                result_to(dst, me).start()

            @pl.when(dst == me)
            def _():
                out[me] = part[me]

    def weigh(c, _):
        query = qs[:, pl.ds(pl.multiple_of(pair_of(c) * wide, wide), wide)]
        score = lax.dot_general(
            ks[...], query, (((0,), (0,)), ((), ())), preferred_element_type=jnp.float32
        )
        top = jnp.max(score, axis=0, keepdims=True)
        probs[c] = jnp.exp2((score - top) * factor).astype(jnp.bfloat16)
        return 0

    lax.fori_loop(0, pairs, weigh, 0)

    place_v(me, v_msg[me])
    for i in range(1, n):
        src = lax.rem(me + n - i, n)
        v_to(src, src).wait_recv()
        place_v(src, v_in[src])

    def finish(c, _):
        first = pair_of(c)
        acc = jnp.dot(vs[...], probs[c], preferred_element_type=jnp.float32)
        done = (acc[:hd] / acc[hd : hd + 1]).astype(jnp.bfloat16)
        part[2 * first] = done[:, :rows]
        part[2 * first + 1] = done[:, rows:]

        @pl.when(c > 0)
        def _():
            send_pair(c - 1)

        return 0

    lax.fori_loop(0, pairs, finish, 0)
    send_pair(pairs - 1)

    for i in range(1, n):
        other = lax.rem(me + i, n)
        kq_to(other, me).wait_send()
        v_to(other, me).wait_send()
        result_to(other, me).wait_send()
        src = lax.rem(me + n - i, n)
        result_to(src, src).wait_recv()


def heads_apart(n, width, tokens, slots, counts, shift, scale, gate, w_qkv, w_out):
    rows = tokens.shape[0]
    hd = width // HEADS
    aug = hd + AUG
    vmem = pl.BlockSpec(memory_space=pltpu.VMEM)
    attended = pl.pallas_call(
        functools.partial(attention, n, hd),
        out_shape=jax.ShapeDtypeStruct((n, hd, rows), jnp.bfloat16),
        in_specs=[vmem] * 5 + [pl.BlockSpec(memory_space=pl.ANY)],
        out_specs=vmem,
        scratch_shapes=[
            pltpu.VMEM((3, width, width), jnp.bfloat16),
            pltpu.VMEM((width, rows), jnp.float32),
            pltpu.VMEM((n, aug + hd, rows), jnp.bfloat16),
            pltpu.VMEM((n, hd, rows), jnp.bfloat16),
            pltpu.VMEM((n, aug + hd, rows), jnp.bfloat16),
            pltpu.VMEM((n, hd, rows), jnp.bfloat16),
            pltpu.VMEM((aug, n * rows), jnp.bfloat16),
            pltpu.VMEM((aug, n * rows), jnp.bfloat16),
            pltpu.VMEM((aug, n * rows), jnp.bfloat16),
            pltpu.VMEM((n // 2, n * rows, 2 * rows), jnp.bfloat16),
            pltpu.VMEM((n, hd, rows), jnp.bfloat16),
            pltpu.SemaphoreType.DMA((3,)),
        ]
        + [pltpu.SemaphoreType.DMA((n,))] * 6,
        compiler_params=pltpu.CompilerParams(
            collective_id=0, has_side_effects=True, vmem_limit_bytes=56 * 1024 * 1024
        ),
    )(slots[None], counts[None], tokens, shift, scale, w_qkv)
    attended = attended.reshape(width, rows)
    onehot = slots[:, None] == jnp.arange(rows, dtype=jnp.int32)[None, :]
    picked = lax.dot_general(
        onehot.astype(jnp.bfloat16),
        attended,
        (((1,), (1,)), ((), ())),
        preferred_element_type=jnp.float32,
    ).astype(jnp.bfloat16)
    branch = jnp.dot(picked, w_out, preferred_element_type=jnp.float32)
    return (tokens.astype(jnp.float32) + gate * branch).astype(jnp.bfloat16)


def rows_gathered(tokens, slots, counts, shift, scale, gate, w_qkv, w_out):
    rows, width = tokens.shape
    nblk = rows // BLK
    hd = width // HEADS
    onehot, merged, bias = merge(tokens, slots, counts)
    normed = layer_norm(merged, shift, scale)
    qkv = jnp.dot(normed, w_qkv, preferred_element_type=jnp.float32)
    query, keys, values = (
        qkv[:, i * width : (i + 1) * width].astype(jnp.bfloat16) for i in range(3)
    )
    keys = lax.all_gather(keys, "patch", axis=0, tiled=True).reshape(-1, HEADS, hd)
    values = lax.all_gather(values, "patch", axis=0, tiled=True).reshape(-1, HEADS, hd)
    bias = lax.all_gather(bias, "patch", axis=0, tiled=True)
    query = query.reshape(rows, HEADS, hd)
    score = jnp.einsum("qhe,khe->hqk", query, keys, preferred_element_type=jnp.float32)
    score = score / hd**0.5 + bias[None, None, :]
    probs = jnp.exp(score - jnp.max(score, axis=-1, keepdims=True))
    total = jnp.sum(probs, axis=-1)
    update = jnp.einsum(
        "hqk,khe->hqe", probs.astype(jnp.bfloat16), values, preferred_element_type=jnp.float32
    )
    attended = (update / total[:, :, None]).transpose(1, 0, 2).reshape(rows, width)
    picked = jnp.einsum(
        "bts,bsd->btd",
        onehot.astype(jnp.bfloat16),
        attended.astype(jnp.bfloat16).reshape(nblk, BLK, width),
        preferred_element_type=jnp.float32,
    ).astype(jnp.bfloat16)
    branch = jnp.dot(picked.reshape(rows, width), w_out, preferred_element_type=jnp.float32)
    return (tokens.astype(jnp.float32) + gate * branch).astype(jnp.bfloat16)


def solution(mesh):
    n = mesh.shape["patch"]

    def body(tokens, *rest):
        if n == HEADS and tokens.shape[0] == BLK:
            return heads_apart(n, tokens.shape[1], tokens, *rest)
        return rows_gathered(tokens, *rest)

    return jax.shard_map(
        body,
        mesh=mesh,
        in_specs=(
            P(("batch", "patch"), None),
            P(("batch", "patch")),
            P(("batch", "patch")),
            P(),
            P(),
            P(),
            P(),
            P(),
        ),
        out_specs=P(("batch", "patch"), None),
        check_vma=False,
    )
```

profile of v0, /device:TPU:0, one launch (start us, length us, event | category | flops | bytes accessed | tf_op | source)
XLA Modules:
  0.0 45.4 jit_solution(10814832462270586521)
XLA Ops:
  0.0 0.0 copy-start
  0.8 0.0 copy-start.1
  0.8 0.0 copy-start.2
  0.8 0.0 copy-start.3
  0.8 42.1 %shard_map.82 = bf16[16,72,128]{2,1,0:T(8,128)(2,1)} custom-call(s32[1,128]{1,0:T(1,128)} %bitcast.7, s32[1,1]{1,0:T(1,128)} %bitcast.5.counts, bf16[128,1152]{1,0:T(8,128)(2,1)} %tokens.1, f32[1152]{0:T(1024)} %shift.1, f32[1152]{0:T(1024)} %scale.1, bf16[1152,3456]{1,0:T(8,128)(2,1)} %w_hbm.1), custom_call_target="tpu_custom_call" | custom-call | tf_op jit(solution)/shard_map/pallas_call | solution.py:218
  42.9 0.0 copy-done
  42.9 0.0 copy-done.1
  42.9 0.0 copy-done.2
  42.9 0.0 copy-done.3
  42.9 2.5 %fusion.1 = bf16[128,1152]{1,0:T(8,128)(2,1)} fusion(bf16[1152,1152]{1,0:T(8,128)(2,1)S(1)} %copy-done, bf16[1152,128]{1,0:T(8,128)(2,1)} %bitcast.6, bf16[128,1152]{1,0:T(8,128)(2,1)S(1)} %copy-done.1, f32[1152]{0:T(1024)S(1)} %copy-done.2, s32[128]{0:T(128)S(1)} %copy-done.3), kind=kOutput, calls=%fused_computation.2 | convolution fusion | flops 378241024 | bytes 3544064 | tf_op jit(solution)/shard_map/dot_general | solution.py:250
Async XLA Ops:
  0.0 42.9 %copy-start = (bf16[1152,1152]{1,0:T(8,128)(2,1)S(1)}, bf16[1152,1152]{1,0:T(8,128)(2,1)}, u32[]{:S(2)}) copy-start(bf16[1152,1152]{1,0:T(8,128)(2,1)} %param.15) | copy-start | bytes 7962628
  0.8 42.1 %copy-start.1 = (bf16[128,1152]{1,0:T(8,128)(2,1)S(1)}, bf16[128,1152]{1,0:T(8,128)(2,1)}, u32[]{:S(2)}) copy-start(bf16[128,1152]{1,0:T(8,128)(2,1)} %tokens.1) | copy-start | bytes 884740
  0.8 42.1 %copy-start.2 = (f32[1152]{0:T(1024)S(1)}, f32[1152]{0:T(1024)}, u32[]{:S(2)}) copy-start(f32[1152]{0:T(1024)} %param.13) | copy-start | bytes 13828
  0.8 42.1 %copy-start.3 = (s32[128]{0:T(128)S(1)}, s32[128]{0:T(128)}, u32[]{:S(2)}) copy-start(s32[128]{0:T(128)} %param.9) | copy-start | bytes 1540
where the time goes:
time: 45.5 us; the launch traced here: 45.4 us
  Pallas kernels  42.1 us (93%)
  matrix products  2.45 us (5%)
  between operations  0.87 us (2%)
    pallas_call x1, Pallas kernels, heads_apart(): pl.pallas_call(functools.partial(attention, n, hd), out_shape=jax.ShapeDt...  42.1 us
    dot_general x1, matrix products, heads_apart(): branch = jnp.dot(picked, w_out, preferred_element_type=jnp.float32)  2.45 us

commit v1 on v0

--- a/solution.py
+++ b/solution.py
@@ -43,19 +43,29 @@
     return onehot, merged, bias
 
 
+def flip(a, mask):
+    out, bit = a, 1
+    while bit <= mask:
+        if mask & bit:
+            out = out + bit * (1 - 2 * lax.rem(lax.div(a, bit), 2))
+        bit *= 2
+    return out
+
+
 def attention(
-    n, hd, slots, counts, tokens, shift, scale, w_hbm, out, w, turned, kq_msg, v_msg,
-    kq_in, v_in, qs, ks, vs, probs, part, w_sem, *sems
+    n, hd, slots, counts, tokens, shift, scale, w_hbm, out, w, turned, kv_msg, q_msg,
+    kv_in, q_in, qs, ks, vs, scores, part, w_sem, *sems
 ):
-    kq_out_sem, kq_in_sem, v_out_sem, v_in_sem, r_out_sem, r_in_sem = sems
+    kv_out_sem, kv_in_sem, q_out_sem, q_in_sem, r_out_sem, r_in_sem = sems
     me = lax.axis_index("patch")
     rows, width = tokens.shape
     aug = hd + AUG
+    factor = math.log2(math.e) / math.sqrt(hd)
 
     def weights(p):
         return pltpu.make_async_copy(w_hbm.at[:, pl.ds(p * width, width)], w.at[p], w_sem.at[p])
 
-    for p in (1, 0, 2):
+    for p in (1, 2, 0):
         weights(p).start()
     barrier = pltpu.get_barrier_semaphore()
     for i in range(1, n):
@@ -63,8 +73,8 @@
             barrier, inc=1, device_id={"patch": lax.rem(me + i, n)}, device_id_type=MESH
         )
 
-    onehot = slots[...] == lax.broadcasted_iota(jnp.int32, (rows, rows), 0)
-    exact = onehot.astype(jnp.float32)
+    slot = lax.broadcasted_iota(jnp.int32, (rows, rows), 0)
+    exact = (slots[...] == jnp.where(slot < counts[...], slot, 0)).astype(jnp.float32)
     picks = exact.astype(jnp.bfloat16)
     sums = jnp.dot(picks, tokens[...], preferred_element_type=jnp.float32)
     members = jnp.sum(exact, axis=1, keepdims=True)
@@ -77,15 +87,7 @@
         preferred_element_type=jnp.float32,
     )
     alive = lax.broadcasted_iota(jnp.int32, (AUG, rows), 1) < counts[...]
-    lift = jnp.where(alive, jnp.log(jnp.maximum(sizes, 1.0)), -1e30) * math.sqrt(hd)
-    high = lift.astype(jnp.bfloat16).astype(jnp.float32)
-    rest = lift - high
-    middle = rest.astype(jnp.bfloat16).astype(jnp.float32)
-    low = rest - middle
-    line = lax.broadcasted_iota(jnp.int32, (AUG, rows), 0)
-    extra = jnp.where(
-        line == 0, high, jnp.where(line == 1, middle, jnp.where(line == 2, low, 0.0))
-    )
+    sizes = jnp.where(alive, sizes, 0.0)
 
     def project(p):
         weights(p).wait()
@@ -98,10 +100,10 @@
 
     project(1)
     for h in range(n):
-        kq_msg[h, :aug] = jnp.concatenate([head(h), extra], axis=0).astype(jnp.bfloat16)
-    project(0)
+        kv_msg[h, :hd] = head(h).astype(jnp.bfloat16)
+    project(2)
     for h in range(n):
-        kq_msg[h, aug:] = head(h).astype(jnp.bfloat16)
+        kv_msg[h, hd:] = jnp.concatenate([head(h) * sizes[:1], sizes], axis=0).astype(jnp.bfloat16)
 
     def copy(src_ref, dst_ref, send, recv, dst, src):
         return pltpu.make_async_remote_copy(
@@ -113,101 +115,99 @@
             device_id_type=MESH,
         )
 
-    def kq_to(dst, src):
-        return copy(kq_msg, kq_in, kq_out_sem, kq_in_sem, dst, src)
-
-    def v_to(dst, src):
-        return copy(v_msg, v_in, v_out_sem, v_in_sem, dst, src)
+    def kv_to(dst, src):
+        return copy(kv_msg, kv_in, kv_out_sem, kv_in_sem, dst, src)
+
+    def q_to(dst, src):
+        return copy(q_msg, q_in, q_out_sem, q_in_sem, dst, src)
 
     def result_to(dst, src):
         return copy(part, out, r_out_sem, r_in_sem, dst, src)
 
     pl.semaphore_wait(barrier, n - 1)
+    for i in range(n - 1, 0, -1):
+        kv_to(flip(me, i), me).start()
+    project(0)
+    for h in range(n):
+        q_msg[h] = (head(h) * factor).astype(jnp.bfloat16)
+    for i in range(n - 1, 0, -1):
+        q_to(flip(me, i), me).start()
+
+    def span(index, size):
+        return pl.ds(pl.multiple_of(index * size, size), size)
+
+    def place_kv(src, block):
+        ks[span(src, rows)] = block[:hd].astype(jnp.float32).T.astype(jnp.bfloat16)
+        vs[:, span(src, rows)] = block[hd:]
+
+    place_kv(me, kv_msg[me])
     for i in range(1, n):
-        kq_to(lax.rem(me + i, n), me).start()
-    project(2)
-    for h in range(n):
-        v_msg[h] = head(h).astype(jnp.bfloat16)
-    for i in range(1, n):
-        v_to(lax.rem(me + i, n), me).start()
-
-    tail = jnp.ones((AUG, rows), jnp.bfloat16)
-
-    def columns(src):
-        return pl.ds(pl.multiple_of(src * rows, rows), rows)
-
-    def place_kq(src, block):
-        ks[:, columns(src)] = block[:aug]
-        qs[:, columns(src)] = jnp.concatenate([block[aug:], tail], axis=0)
-
-    def place_v(src, block):
-        vs[:, columns(src)] = jnp.concatenate([block, tail], axis=0)
-
-    place_kq(me, kq_msg[me])
-    for i in range(1, n):
-        src = lax.rem(me + n - i, n)
-        kq_to(src, src).wait_recv()
-        place_kq(src, kq_in[src])
-
-    factor = math.log2(math.e) / math.sqrt(hd)
+        src = flip(me, i)
+        kv_to(src, src).wait_recv()
+        place_kv(src, kv_in[src])
+
     wide = 2 * rows
     pairs = n // 2
+    total = n * rows
+    mine = lax.div(me, 2)
 
     def pair_of(c):
-        return lax.rem(me // 2 + c, pairs)
-
-    def send_pair(c):
+        return flip(mine, c)
+
+    def gather_queries(c):
         for t in range(2):
-            dst = 2 * pair_of(c) + t
-
-            @pl.when(dst != me)
+            src = 2 * pair_of(c) + t
+
+            @pl.when(src != me)
             def _():
-                result_to(dst, me).start()
-
-            @pl.when(dst == me)
+                q_to(src, src).wait_recv()
+                qs[c % 2, :, t * rows : (t + 1) * rows] = q_in[src]
+
+            @pl.when(src == me)
             def _():
-                out[me] = part[me]
-
-    def weigh(c, _):
-        query = qs[:, pl.ds(pl.multiple_of(pair_of(c) * wide, wide), wide)]
-        score = lax.dot_general(
-            ks[...], query, (((0,), (0,)), ((), ())), preferred_element_type=jnp.float32
-        )
-        top = jnp.max(score, axis=0, keepdims=True)
-        probs[c] = jnp.exp2((score - top) * factor).astype(jnp.bfloat16)
-        return 0
-
-    lax.fori_loop(0, pairs, weigh, 0)
-
-    place_v(me, v_msg[me])
+                qs[c % 2, :, t * rows : (t + 1) * rows] = q_msg[me]
+
+    def step(c, top):
+        peak = jnp.full((8, wide), -jnp.inf, jnp.float32)
+        acc = jnp.zeros((aug, wide), jnp.float32)
+        for at in range(0, total, wide):
+            if c + 1 < pairs:
+                score = jnp.dot(
+                    ks[at : at + wide], qs[(c + 1) % 2], preferred_element_type=jnp.float32
+                )
+                scores[(c + 1) % 2, at : at + wide] = score
+                peak = jnp.maximum(peak, jnp.max(score.reshape(wide // 8, 8, wide), axis=0))
+            if c >= 0:
+                probs = jnp.exp2(scores[c % 2, at : at + wide] - top).astype(jnp.bfloat16)
+                acc += jnp.dot(vs[:, at : at + wide], probs, preferred_element_type=jnp.float32)
+        if c >= 0:
+            done = (acc[:hd] / acc[hd : hd + 1]).astype(jnp.bfloat16)
+            for t in range(2):
+                dst = 2 * pair_of(c) + t
+                part[dst] = done[:, t * rows : (t + 1) * rows]
+
+                @pl.when(dst != me)
+                def _():
+                    result_to(dst, me).start()
+
+                @pl.when(dst == me)
+                def _():
+                    out[me] = part[me]
+
+        return jnp.max(peak, axis=0, keepdims=True)
+
+    top = None
+    for c in range(-1, pairs):
+        if c + 1 < pairs:
+            gather_queries(c + 1)
+        top = step(c, top)
+
     for i in range(1, n):
-        src = lax.rem(me + n - i, n)
-        v_to(src, src).wait_recv()
-        place_v(src, v_in[src])
-
-    def finish(c, _):
-        first = pair_of(c)
-        acc = jnp.dot(vs[...], probs[c], preferred_element_type=jnp.float32)
-        done = (acc[:hd] / acc[hd : hd + 1]).astype(jnp.bfloat16)
-        part[2 * first] = done[:, :rows]
-        part[2 * first + 1] = done[:, rows:]
-
-        @pl.when(c > 0)
-        def _():
-            send_pair(c - 1)
-
-        return 0
-
-    lax.fori_loop(0, pairs, finish, 0)
-    send_pair(pairs - 1)
-
-    for i in range(1, n):
-        other = lax.rem(me + i, n)
-        kq_to(other, me).wait_send()
-        v_to(other, me).wait_send()
+        other = flip(me, i)
+        kv_to(other, me).wait_send()
+        q_to(other, me).wait_send()
         result_to(other, me).wait_send()
-        src = lax.rem(me + n - i, n)
-        result_to(src, src).wait_recv()
+        result_to(other, other).wait_recv()
 
 
 def heads_apart(n, width, tokens, slots, counts, shift, scale, gate, w_qkv, w_out):
@@ -223,14 +223,14 @@
         scratch_shapes=[
             pltpu.VMEM((3, width, width), jnp.bfloat16),
             pltpu.VMEM((width, rows), jnp.float32),
-            pltpu.VMEM((n, aug + hd, rows), jnp.bfloat16),
+            pltpu.VMEM((n, hd + aug, rows), jnp.bfloat16),
             pltpu.VMEM((n, hd, rows), jnp.bfloat16),
-            pltpu.VMEM((n, aug + hd, rows), jnp.bfloat16),
+            pltpu.VMEM((n, hd + aug, rows), jnp.bfloat16),
             pltpu.VMEM((n, hd, rows), jnp.bfloat16),
+            pltpu.VMEM((2, hd, 2 * rows), jnp.bfloat16),
+            pltpu.VMEM((n * rows, hd), jnp.bfloat16),
             pltpu.VMEM((aug, n * rows), jnp.bfloat16),
-            pltpu.VMEM((aug, n * rows), jnp.bfloat16),
-            pltpu.VMEM((aug, n * rows), jnp.bfloat16),
-            pltpu.VMEM((n // 2, n * rows, 2 * rows), jnp.bfloat16),
+            pltpu.VMEM((2, n * rows, 2 * rows), jnp.float32),
             pltpu.VMEM((n, hd, rows), jnp.bfloat16),
             pltpu.SemaphoreType.DMA((3,)),
         ]

time: 45.5 us -> 42.7 us (0.938)
  Pallas kernels: 42.1 us -> 39.3 us
    pallas_call x1, Pallas kernels: 42.1 us -> 39.3 us  [heads_apart(): pl.pallas_call(functools.partial(attention, n, hd), out_shape=jax.ShapeDt...]
where the time goes in v1:
time: 42.7 us; the launch traced here: 42.6 us
  Pallas kernels  39.3 us (92%)
  matrix products  2.45 us (6%)
  between operations  0.87 us (2%)
    pallas_call x1, Pallas kernels, heads_apart(): pl.pallas_call(functools.partial(attention, n, hd), out_shape=jax.ShapeDt...  39.3 us
    dot_general x1, matrix products, heads_apart(): branch = jnp.dot(picked, w_out, preferred_element_type=jnp.float32)  2.45 us

profile of v1, /device:TPU:0, one launch (start us, length us, event | category | flops | bytes accessed | tf_op | source)
XLA Modules:
  0.0 42.6 jit_solution(3272248797430532157)
XLA Ops:
  0.0 0.0 copy-start
  0.8 0.0 copy-start.1
  0.8 0.0 copy-start.2
  0.8 0.0 copy-start.3
  0.8 39.3 %shard_map.82 = bf16[16,72,128]{2,1,0:T(8,128)(2,1)} custom-call(s32[1,128]{1,0:T(1,128)} %bitcast.7, s32[1,1]{1,0:T(1,128)} %bitcast.5.counts, bf16[128,1152]{1,0:T(8,128)(2,1)} %tokens.1, f32[1152]{0:T(1024)} %shift.1, f32[1152]{0:T(1024)} %scale.1, bf16[1152,3456]{1,0:T(8,128)(2,1)} %w_hbm.1), custom_call_target="tpu_custom_call" | custom-call | tf_op jit(solution)/shard_map/pallas_call | solution.py:218
  40.1 0.0 copy-done
  40.1 0.0 copy-done.1
  40.1 0.0 copy-done.2
  40.1 0.0 copy-done.3
  40.1 2.5 %fusion.1 = bf16[128,1152]{1,0:T(8,128)(2,1)} fusion(bf16[1152,1152]{1,0:T(8,128)(2,1)S(1)} %copy-done, bf16[1152,128]{1,0:T(8,128)(2,1)} %bitcast.6, bf16[128,1152]{1,0:T(8,128)(2,1)S(1)} %copy-done.1, f32[1152]{0:T(1024)S(1)} %copy-done.2, s32[128]{0:T(128)S(1)} %copy-done.3), kind=kOutput, calls=%fused_computation.2 | convolution fusion | flops 378241024 | bytes 3544064 | tf_op jit(solution)/shard_map/dot_general | solution.py:250
Async XLA Ops:
  0.0 40.1 %copy-start = (bf16[1152,1152]{1,0:T(8,128)(2,1)S(1)}, bf16[1152,1152]{1,0:T(8,128)(2,1)}, u32[]{:S(2)}) copy-start(bf16[1152,1152]{1,0:T(8,128)(2,1)} %param.15) | copy-start | bytes 7962628
  0.8 39.3 %copy-start.1 = (bf16[128,1152]{1,0:T(8,128)(2,1)S(1)}, bf16[128,1152]{1,0:T(8,128)(2,1)}, u32[]{:S(2)}) copy-start(bf16[128,1152]{1,0:T(8,128)(2,1)} %tokens.1) | copy-start | bytes 884740
  0.8 39.3 %copy-start.2 = (f32[1152]{0:T(1024)S(1)}, f32[1152]{0:T(1024)}, u32[]{:S(2)}) copy-start(f32[1152]{0:T(1024)} %param.13) | copy-start | bytes 13828
  0.8 39.3 %copy-start.3 = (s32[128]{0:T(128)S(1)}, s32[128]{0:T(128)}, u32[]{:S(2)}) copy-start(s32[128]{0:T(128)} %param.9) | copy-start | bytes 1540

commit v2 on v1

--- a/solution.py
+++ b/solution.py
@@ -53,29 +53,65 @@
 
 
 def attention(
-    n, hd, slots, counts, tokens, shift, scale, w_hbm, out, w, turned, kv_msg, q_msg,
-    kv_in, q_in, qs, ks, vs, scores, part, w_sem, *sems
+    n, hd, slots_hbm, tokens_hbm, shift_hbm, scale_hbm, gate_hbm, w_hbm, wo_hbm, out, slots,
+    tokens, shift, scale, gate, wo, back, r_in, w_far, w_near, turned, kv_msg, q_msg, kv_in, q_in, qs, ks, vs, scores, part,
+    small_sem, w_sem, wo_sem, *sems
 ):
     kv_out_sem, kv_in_sem, q_out_sem, q_in_sem, r_out_sem, r_in_sem = sems
     me = lax.axis_index("patch")
-    rows, width = tokens.shape
+    rows, width = tokens_hbm.shape
     aug = hd + AUG
     factor = math.log2(math.e) / math.sqrt(hd)
 
-    def weights(p):
-        return pltpu.make_async_copy(w_hbm.at[:, pl.ds(p * width, width)], w.at[p], w_sem.at[p])
-
-    for p in (1, 2, 0):
-        weights(p).start()
+    half = n // 2
+    cols = half * hd
+    near_cols = -(-cols // 128) * 128
+    far_cols = width - near_cols
+    side = lax.div(me, half)
+    near_at = pl.multiple_of(side * far_cols, 128)
+    far_at = pl.multiple_of((1 - side) * near_cols, 128)
+
+    def weights(p, far):
+        at, size, dst = (far_at, far_cols, w_far) if far else (near_at, near_cols, w_near)
+        start = pl.multiple_of(p * width + at, 128)
+        return pltpu.make_async_copy(
+            w_hbm.at[:, pl.ds(start, size)], dst.at[p], w_sem.at[2 * p + far]
+        )
+
     barrier = pltpu.get_barrier_semaphore()
-    for i in range(1, n):
+    for i in range(n - 1, 0, -1):
         pl.semaphore_signal(
-            barrier, inc=1, device_id={"patch": lax.rem(me + i, n)}, device_id_type=MESH
+            barrier, inc=1, device_id={"patch": flip(me, i)}, device_id_type=MESH
         )
+    small = [
+        pltpu.make_async_copy(src, dst, small_sem.at[i])
+        for i, (src, dst) in enumerate(
+            (
+                (slots_hbm, slots),
+                (tokens_hbm, tokens),
+                (shift_hbm, shift),
+                (scale_hbm, scale),
+                (gate_hbm, gate),
+            )
+        )
+    ]
+    for item in small:
+        item.start()
+    for far in (0, 1):
+        for p in (1, 2):
+            weights(p, far).start()
+    for far in (0, 1):
+        weights(0, far).start()
+    load_wo = pltpu.make_async_copy(wo_hbm, wo, wo_sem)
+    load_wo.start()
+    for item in small:
+        item.wait()
 
     slot = lax.broadcasted_iota(jnp.int32, (rows, rows), 0)
-    exact = (slots[...] == jnp.where(slot < counts[...], slot, 0)).astype(jnp.float32)
+    live = jnp.max(slots[...][None], axis=1, keepdims=True) + 1
+    exact = (slots[...][None] == jnp.where(slot < live, slot, 0)).astype(jnp.float32)
     picks = exact.astype(jnp.bfloat16)
+    back[...] = (slots[...][None] == slot).astype(jnp.float32).T.astype(jnp.bfloat16)
     sums = jnp.dot(picks, tokens[...], preferred_element_type=jnp.float32)
     members = jnp.sum(exact, axis=1, keepdims=True)
     merged = (sums / jnp.maximum(members, 1.0)).astype(jnp.bfloat16)
@@ -86,24 +122,36 @@
         (((1,), (1,)), ((), ())),
         preferred_element_type=jnp.float32,
     )
-    alive = lax.broadcasted_iota(jnp.int32, (AUG, rows), 1) < counts[...]
+    alive = lax.broadcasted_iota(jnp.int32, (AUG, rows), 1) < live
     sizes = jnp.where(alive, sizes, 0.0)
 
-    def project(p):
-        weights(p).wait()
-        for at in range(0, width, CHUNK):
-            piece = jnp.dot(normed, w[p, :, at : at + CHUNK], preferred_element_type=jnp.float32)
-            turned[at : at + CHUNK] = piece.T
-
-    def head(h):
-        return turned[h * hd : (h + 1) * hd]
-
-    project(1)
-    for h in range(n):
-        kv_msg[h, :hd] = head(h).astype(jnp.bfloat16)
-    project(2)
-    for h in range(n):
-        kv_msg[h, hd:] = jnp.concatenate([head(h) * sizes[:1], sizes], axis=0).astype(jnp.bfloat16)
+    def project(p, far):
+        weights(p, far).wait()
+        at, size, src = (far_at, far_cols, w_far) if far else (near_at, near_cols, w_near)
+        piece = jnp.dot(normed, src[p], preferred_element_type=jnp.float32)
+        turned[pl.ds(p * width + at, size)] = piece.T
+
+    def heads(far):
+        base = ((1 - side) if far else side) * half
+        return [base + j for j in range(half)]
+
+    def head(p, h):
+        return turned[pl.ds(pl.multiple_of(p * width + h * hd, 8), hd)]
+
+    def pack_kv(far):
+        for h in heads(far):
+            kv_msg[h, :hd] = head(1, h).astype(jnp.bfloat16)
+            kv_msg[h, hd:] = jnp.concatenate([head(2, h) * sizes[:1], sizes], axis=0).astype(
+                jnp.bfloat16
+            )
+
+    def pack_q(far):
+        for h in heads(far):
+            q_msg[h] = (head(0, h) * factor).astype(jnp.bfloat16)
+
+    project(1, 0)
+    project(2, 0)
+    pack_kv(0)
 
     def copy(src_ref, dst_ref, send, recv, dst, src):
         return pltpu.make_async_remote_copy(
@@ -122,17 +170,24 @@
         return copy(q_msg, q_in, q_out_sem, q_in_sem, dst, src)
 
     def result_to(dst, src):
-        return copy(part, out, r_out_sem, r_in_sem, dst, src)
+        return copy(part, r_in, r_out_sem, r_in_sem, dst, src)
 
     pl.semaphore_wait(barrier, n - 1)
-    for i in range(n - 1, 0, -1):
+    for i in range(1, half):
         kv_to(flip(me, i), me).start()
-    project(0)
-    for h in range(n):
-        q_msg[h] = (head(h) * factor).astype(jnp.bfloat16)
-    for i in range(n - 1, 0, -1):
+    project(1, 1)
+    project(2, 1)
+    pack_kv(1)
+    for i in range(half, n):
+        kv_to(flip(me, i), me).start()
+    project(0, 0)
+    pack_q(0)
+    for i in range(1, half):
         q_to(flip(me, i), me).start()
-
+    project(0, 1)
+    pack_q(1)
+    for i in range(half, n):
+        q_to(flip(me, i), me).start()
     def span(index, size):
         return pl.ds(pl.multiple_of(index * size, size), size)
 
@@ -192,7 +247,7 @@
 
                 @pl.when(dst == me)
                 def _():
-                    out[me] = part[me]
+                    r_in[me] = part[me]
 
         return jnp.max(peak, axis=0, keepdims=True)
 
@@ -202,27 +257,52 @@
             gather_queries(c + 1)
         top = step(c, top)
 
+    load_wo.wait()
+    branch = jnp.zeros((rows, width), jnp.float32)
+    deep = 2 * hd
+    for c in range(pairs):
+        pair = pair_of(c)
+        for t in range(2):
+            src = flip(me, 2 * c + t)
+            if 2 * c + t:
+                result_to(src, src).wait_recv()
+        heads_in = jnp.concatenate([r_in[2 * pair], r_in[2 * pair + 1]], axis=0)
+        picked = lax.dot_general(
+            back[...], heads_in, (((1,), (1,)), ((), ())), preferred_element_type=jnp.float32
+        ).astype(jnp.bfloat16)
+        branch += jnp.dot(picked, wo[span(pair, deep)], preferred_element_type=jnp.float32)
+    out[...] = (tokens[...].astype(jnp.float32) + gate[...][None] * branch).astype(jnp.bfloat16)
+
     for i in range(1, n):
         other = flip(me, i)
         kv_to(other, me).wait_send()
         q_to(other, me).wait_send()
         result_to(other, me).wait_send()
-        result_to(other, other).wait_recv()
 
 
 def heads_apart(n, width, tokens, slots, counts, shift, scale, gate, w_qkv, w_out):
     rows = tokens.shape[0]
     hd = width // HEADS
     aug = hd + AUG
+    far_cols = width - -(-(n // 2 * hd) // 128) * 128
     vmem = pl.BlockSpec(memory_space=pltpu.VMEM)
-    attended = pl.pallas_call(
+    return pl.pallas_call(
         functools.partial(attention, n, hd),
-        out_shape=jax.ShapeDtypeStruct((n, hd, rows), jnp.bfloat16),
-        in_specs=[vmem] * 5 + [pl.BlockSpec(memory_space=pl.ANY)],
+        out_shape=pltpu.VMEM((rows, width), jnp.bfloat16),
+        in_specs=[pl.BlockSpec(memory_space=pltpu.HBM)] * 7,
         out_specs=vmem,
         scratch_shapes=[
-            pltpu.VMEM((3, width, width), jnp.bfloat16),
-            pltpu.VMEM((width, rows), jnp.float32),
+            pltpu.VMEM((rows,), jnp.int32),
+            pltpu.VMEM((rows, width), jnp.bfloat16),
+            pltpu.VMEM((width,), jnp.float32),
+            pltpu.VMEM((width,), jnp.float32),
+            pltpu.VMEM((width,), jnp.float32),
+            pltpu.VMEM((width, width), jnp.bfloat16),
+            pltpu.VMEM((rows, rows), jnp.bfloat16),
+            pltpu.VMEM((n, hd, rows), jnp.bfloat16),
+            pltpu.VMEM((3, width, far_cols), jnp.bfloat16),
+            pltpu.VMEM((3, width, width - far_cols), jnp.bfloat16),
+            pltpu.VMEM((3 * width, rows), jnp.float32),
             pltpu.VMEM((n, hd + aug, rows), jnp.bfloat16),
             pltpu.VMEM((n, hd, rows), jnp.bfloat16),
             pltpu.VMEM((n, hd + aug, rows), jnp.bfloat16),
@@ -232,23 +312,15 @@
             pltpu.VMEM((aug, n * rows), jnp.bfloat16),
             pltpu.VMEM((2, n * rows, 2 * rows), jnp.float32),
             pltpu.VMEM((n, hd, rows), jnp.bfloat16),
-            pltpu.SemaphoreType.DMA((3,)),
+            pltpu.SemaphoreType.DMA((5,)),
+            pltpu.SemaphoreType.DMA((6,)),
+            pltpu.SemaphoreType.DMA,
         ]
         + [pltpu.SemaphoreType.DMA((n,))] * 6,
         compiler_params=pltpu.CompilerParams(
-            collective_id=0, has_side_effects=True, vmem_limit_bytes=56 * 1024 * 1024
+            collective_id=0, has_side_effects=True, vmem_limit_bytes=57 * 1024 * 1024
         ),
-    )(slots[None], counts[None], tokens, shift, scale, w_qkv)
-    attended = attended.reshape(width, rows)
-    onehot = slots[:, None] == jnp.arange(rows, dtype=jnp.int32)[None, :]
-    picked = lax.dot_general(
-        onehot.astype(jnp.bfloat16),
-        attended,
-        (((1,), (1,)), ((), ())),
-        preferred_element_type=jnp.float32,
-    ).astype(jnp.bfloat16)
-    branch = jnp.dot(picked, w_out, preferred_element_type=jnp.float32)
-    return (tokens.astype(jnp.float32) + gate * branch).astype(jnp.bfloat16)
+    )(slots, tokens, shift, scale, gate, w_qkv, w_out)
 
 
 def rows_gathered(tokens, slots, counts, shift, scale, gate, w_qkv, w_out):

time: 42.7 us -> 40.6 us (0.951)
  matrix products: 2.45 us -> 0 us
  between operations: 0.87 us -> 0.01 us
  local copies, waits for them, and re-layouts: 0.02 us -> 0.72 us
    dot_general x1 -> x0, matrix products: 2.45 us -> none  [heads_apart(): branch = jnp.dot(picked, w_out, preferred_element_type=jnp.float32)]
    unnamed x8 -> x1, local copies, waits for them, and re-layouts: 0.02 us -> 0.72 us
    pallas_call x1, Pallas kernels: 39.3 us -> 39.7 us  [heads_apart(): pl.pallas_call(functools.partial(attention, n, hd), out_shape=pltpu.VMEM(...]
where the time goes in v2:
time: 40.6 us; the launch traced here: 40.4 us
  Pallas kernels  39.7 us (98%)
  local copies, waits for them, and re-layouts  0.72 us (2%)
    pallas_call x1, Pallas kernels, heads_apart(): pl.pallas_call(functools.partial(attention, n, hd), out_shape=pltpu.VMEM(...  39.7 us

profile of v2, /device:TPU:0, one launch (start us, length us, event | category | flops | bytes accessed | tf_op | source)
XLA Modules:
  0.0 40.4 jit_solution(4648733903865104205)
XLA Ops:
  0.0 39.7 %shard_map.73 = bf16[128,1152]{1,0:T(8,128)(2,1)S(1)} custom-call(s32[128]{0:T(128)} %slots_hbm.1, bf16[128,1152]{1,0:T(8,128)(2,1)} %tokens_hbm.1, f32[1152]{0:T(1024)} %shift_hbm.1, f32[1152]{0:T(1024)} %scale_hbm.1, f32[1152]{0:T(1024)} %gate_hbm.1, bf16[1152,3456]{1,0:T(8,128)(2,1)} %w_hbm.1, bf16[1152,1152]{1,0:T(8,128)(2,1)} %wo_hbm.1), custom_call_target="tpu_custom_call" | custom-call | tf_op jit(solution)/shard_map/pallas_call | solution.py:289
  39.7 0.7 %copy.9 = bf16[128,1152]{1,0:T(8,128)(2,1)} copy(bf16[128,1152]{1,0:T(8,128)(2,1)S(1)} %shard_map.73) | data formatting | bytes 589824

commit v3 on v2

--- a/solution.py
+++ b/solution.py
@@ -54,10 +54,11 @@
 
 def attention(
     n, hd, slots_hbm, tokens_hbm, shift_hbm, scale_hbm, gate_hbm, w_hbm, wo_hbm, out, slots,
-    tokens, shift, scale, gate, wo, back, r_in, w_far, w_near, turned, kv_msg, q_msg, kv_in, q_in, qs, ks, vs, scores, part,
+    tokens, shift, scale, gate, wo, back, r_in, w_broad, w_slim, turned, k_msg, v_msg, q_msg, m_msg, k_in, v_in, q_in, m_in,
+    qs, ks, vs, scores, part,
     small_sem, w_sem, wo_sem, *sems
 ):
-    kv_out_sem, kv_in_sem, q_out_sem, q_in_sem, r_out_sem, r_in_sem = sems
+    k_sems, v_sems, q_sems, m_sems, r_sems = (sems[i : i + 2] for i in range(0, 10, 2))
     me = lax.axis_index("patch")
     rows, width = tokens_hbm.shape
     aug = hd + AUG
@@ -65,18 +66,20 @@
 
     half = n // 2
     cols = half * hd
-    near_cols = -(-cols // 128) * 128
-    far_cols = width - near_cols
+    broad = -(-cols // 128) * 128
+    slim = width - broad
     side = lax.div(me, half)
-    near_at = pl.multiple_of(side * far_cols, 128)
-    far_at = pl.multiple_of((1 - side) * near_cols, 128)
+
+    def chunk(p, far):
+        early = (0, 1, 1)[p] == far
+        size, buf = (broad, w_broad) if early else (slim, w_slim)
+        at = ((1 - side) if far else side) * (width - size)
+        return pl.multiple_of(at, 128), size, buf.at[p]
 
     def weights(p, far):
-        at, size, dst = (far_at, far_cols, w_far) if far else (near_at, near_cols, w_near)
+        at, size, buf = chunk(p, far)
         start = pl.multiple_of(p * width + at, 128)
-        return pltpu.make_async_copy(
-            w_hbm.at[:, pl.ds(start, size)], dst.at[p], w_sem.at[2 * p + far]
-        )
+        return pltpu.make_async_copy(w_hbm.at[:, pl.ds(start, size)], buf, w_sem.at[2 * p + far])
 
     barrier = pltpu.get_barrier_semaphore()
     for i in range(n - 1, 0, -1):
@@ -97,11 +100,8 @@
     ]
     for item in small:
         item.start()
-    for far in (0, 1):
-        for p in (1, 2):
-            weights(p, far).start()
-    for far in (0, 1):
-        weights(0, far).start()
+    for p, far in ((1, 1), (1, 0), (2, 1), (2, 0), (0, 0), (0, 1)):
+        weights(p, far).start()
     load_wo = pltpu.make_async_copy(wo_hbm, wo, wo_sem)
     load_wo.start()
     for item in small:
@@ -124,11 +124,12 @@
     )
     alive = lax.broadcasted_iota(jnp.int32, (AUG, rows), 1) < live
     sizes = jnp.where(alive, sizes, 0.0)
+    m_msg[...] = sizes[:1]
 
     def project(p, far):
         weights(p, far).wait()
-        at, size, src = (far_at, far_cols, w_far) if far else (near_at, near_cols, w_near)
-        piece = jnp.dot(normed, src[p], preferred_element_type=jnp.float32)
+        at, size, buf = chunk(p, far)
+        piece = jnp.dot(normed, buf[...], preferred_element_type=jnp.float32)
         turned[pl.ds(p * width + at, size)] = piece.T
 
     def heads(far):
@@ -138,76 +139,91 @@
     def head(p, h):
         return turned[pl.ds(pl.multiple_of(p * width + h * hd, 8), hd)]
 
-    def pack_kv(far):
+    def pack(p, far):
+        project(p, far)
         for h in heads(far):
-            kv_msg[h, :hd] = head(1, h).astype(jnp.bfloat16)
-            kv_msg[h, hd:] = jnp.concatenate([head(2, h) * sizes[:1], sizes], axis=0).astype(
-                jnp.bfloat16
-            )
-
-    def pack_q(far):
-        for h in heads(far):
-            q_msg[h] = (head(0, h) * factor).astype(jnp.bfloat16)
-
-    project(1, 0)
-    project(2, 0)
-    pack_kv(0)
-
-    def copy(src_ref, dst_ref, send, recv, dst, src):
+            if p == 0:
+                q_msg[h] = (head(0, h) * factor).astype(jnp.bfloat16)
+            elif p == 1:
+                k_msg[h] = head(1, h).astype(jnp.bfloat16)
+            else:
+                v_msg[h] = (head(2, h) * sizes[:1]).astype(jnp.bfloat16)
+
+    def copy(src_ref, dst_ref, sems, dst, src):
         return pltpu.make_async_remote_copy(
-            src_ref=src_ref.at[dst],
+            src_ref=src_ref,
             dst_ref=dst_ref.at[src],
-            send_sem=send.at[dst],
-            recv_sem=recv.at[src],
+            send_sem=sems[0].at[dst],
+            recv_sem=sems[1].at[src],
             device_id={"patch": dst},
             device_id_type=MESH,
         )
 
-    def kv_to(dst, src):
-        return copy(kv_msg, kv_in, kv_out_sem, kv_in_sem, dst, src)
+    def k_to(dst, src):
+        return copy(k_msg.at[dst], k_in, k_sems, dst, src)
+
+    def v_to(dst, src):
+        return copy(v_msg.at[dst], v_in, v_sems, dst, src)
 
     def q_to(dst, src):
-        return copy(q_msg, q_in, q_out_sem, q_in_sem, dst, src)
+        return copy(q_msg.at[dst], q_in, q_sems, dst, src)
+
+    def m_to(dst, src):
+        return copy(m_msg, m_in, m_sems, dst, src)
 
     def result_to(dst, src):
-        return copy(part, r_in, r_out_sem, r_in_sem, dst, src)
-
+        return copy(part.at[dst], r_in, r_sems, dst, src)
+
+    def send(to, far):
+        for i in range(half, n) if far else range(1, half):
+            to(flip(me, i), me).start()
+
+    pack(1, 1)
     pl.semaphore_wait(barrier, n - 1)
-    for i in range(1, half):
-        kv_to(flip(me, i), me).start()
-    project(1, 1)
-    project(2, 1)
-    pack_kv(1)
-    for i in range(half, n):
-        kv_to(flip(me, i), me).start()
-    project(0, 0)
-    pack_q(0)
-    for i in range(1, half):
-        q_to(flip(me, i), me).start()
-    project(0, 1)
-    pack_q(1)
-    for i in range(half, n):
-        q_to(flip(me, i), me).start()
+    send(k_to, 1)
+    send(m_to, 1)
+    pack(1, 0)
+    send(k_to, 0)
+    send(m_to, 0)
+    pack(2, 1)
+    send(v_to, 1)
+    pack(2, 0)
+    send(v_to, 0)
+    pack(0, 0)
+    send(q_to, 0)
+    pack(0, 1)
+    send(q_to, 1)
+
     def span(index, size):
         return pl.ds(pl.multiple_of(index * size, size), size)
 
-    def place_kv(src, block):
-        ks[span(src, rows)] = block[:hd].astype(jnp.float32).T.astype(jnp.bfloat16)
-        vs[:, span(src, rows)] = block[hd:]
-
-    place_kv(me, kv_msg[me])
+    def place_k(src, block):
+        ks[span(src, rows)] = block.astype(jnp.float32).T.astype(jnp.bfloat16)
+
+    def place_v(src, block, size):
+        vs[:hd, span(src, rows)] = block
+        vs[hd:, span(src, rows)] = jnp.broadcast_to(size, (AUG, rows)).astype(jnp.bfloat16)
+
+    place_k(me, k_msg[me])
+    place_v(me, v_msg[me], m_msg[...])
     for i in range(1, n):
         src = flip(me, i)
-        kv_to(src, src).wait_recv()
-        place_kv(src, kv_in[src])
+        k_to(src, src).wait_recv()
+        place_k(src, k_in[src])
+    for i in range(1, n):
+        src = flip(me, i)
+        m_to(src, src).wait_recv()
+        v_to(src, src).wait_recv()
+        place_v(src, v_in[src], m_in[src])
 
     wide = 2 * rows
     pairs = n // 2
     total = n * rows
     mine = lax.div(me, 2)
+    turn = [pairs // 2 * (c % 2) + c // 2 for c in range(pairs)]
 
     def pair_of(c):
-        return flip(mine, c)
+        return flip(mine, turn[c])
 
     def gather_queries(c):
         for t in range(2):
@@ -263,8 +279,8 @@
     for c in range(pairs):
         pair = pair_of(c)
         for t in range(2):
-            src = flip(me, 2 * c + t)
-            if 2 * c + t:
+            src = flip(me, 2 * turn[c] + t)
+            if 2 * turn[c] + t:
                 result_to(src, src).wait_recv()
         heads_in = jnp.concatenate([r_in[2 * pair], r_in[2 * pair + 1]], axis=0)
         picked = lax.dot_general(
@@ -275,7 +291,9 @@
 
     for i in range(1, n):
         other = flip(me, i)
-        kv_to(other, me).wait_send()
+        k_to(other, me).wait_send()
+        v_to(other, me).wait_send()
+        m_to(other, me).wait_send()
         q_to(other, me).wait_send()
         result_to(other, me).wait_send()
 
@@ -284,7 +302,7 @@
     rows = tokens.shape[0]
     hd = width // HEADS
     aug = hd + AUG
-    far_cols = width - -(-(n // 2 * hd) // 128) * 128
+    broad = -(-(n // 2 * hd) // 128) * 128
     vmem = pl.BlockSpec(memory_space=pltpu.VMEM)
     return pl.pallas_call(
         functools.partial(attention, n, hd),
@@ -300,13 +318,17 @@
             pltpu.VMEM((width, width), jnp.bfloat16),
             pltpu.VMEM((rows, rows), jnp.bfloat16),
             pltpu.VMEM((n, hd, rows), jnp.bfloat16),
-            pltpu.VMEM((3, width, far_cols), jnp.bfloat16),
-            pltpu.VMEM((3, width, width - far_cols), jnp.bfloat16),
+            pltpu.VMEM((3, width, broad), jnp.bfloat16),
+            pltpu.VMEM((3, width, width - broad), jnp.bfloat16),
             pltpu.VMEM((3 * width, rows), jnp.float32),
-            pltpu.VMEM((n, hd + aug, rows), jnp.bfloat16),
-            pltpu.VMEM((n, hd, rows), jnp.bfloat16),
-            pltpu.VMEM((n, hd + aug, rows), jnp.bfloat16),
-            pltpu.VMEM((n, hd, rows), jnp.bfloat16),
+            pltpu.VMEM((n, hd, rows), jnp.bfloat16),
+            pltpu.VMEM((n, hd, rows), jnp.bfloat16),
+            pltpu.VMEM((n, hd, rows), jnp.bfloat16),
+            pltpu.VMEM((1, rows), jnp.float32),
+            pltpu.VMEM((n, hd, rows), jnp.bfloat16),
+            pltpu.VMEM((n, hd, rows), jnp.bfloat16),
+            pltpu.VMEM((n, hd, rows), jnp.bfloat16),
+            pltpu.VMEM((n, 1, rows), jnp.float32),
             pltpu.VMEM((2, hd, 2 * rows), jnp.bfloat16),
             pltpu.VMEM((n * rows, hd), jnp.bfloat16),
             pltpu.VMEM((aug, n * rows), jnp.bfloat16),
@@ -316,7 +338,7 @@
             pltpu.SemaphoreType.DMA((6,)),
             pltpu.SemaphoreType.DMA,
         ]
-        + [pltpu.SemaphoreType.DMA((n,))] * 6,
+        + [pltpu.SemaphoreType.DMA((n,))] * 10,
         compiler_params=pltpu.CompilerParams(
             collective_id=0, has_side_effects=True, vmem_limit_bytes=57 * 1024 * 1024
         ),

time: 40.6 us -> 39.3 us (0.968)
  Pallas kernels: 39.7 us -> 38.5 us
    pallas_call x1, Pallas kernels: 39.7 us -> 38.5 us  [heads_apart(): pl.pallas_call(functools.partial(attention, n, hd), out_shape=pltpu.VMEM(...]
where the time goes in v3:
time: 39.3 us; the launch traced here: 39.2 us
  Pallas kernels  38.5 us (98%)
  local copies, waits for them, and re-layouts  0.72 us (2%)
    pallas_call x1, Pallas kernels, heads_apart(): pl.pallas_call(functools.partial(attention, n, hd), out_shape=pltpu.VMEM(...  38.5 us

profile of v3, /device:TPU:0, one launch (start us, length us, event | category | flops | bytes accessed | tf_op | source)
XLA Modules:
  0.0 39.2 jit_solution(4581900205953694307)
XLA Ops:
  0.0 38.5 %shard_map.73 = bf16[128,1152]{1,0:T(8,128)(2,1)S(1)} custom-call(s32[128]{0:T(128)} %slots_hbm.1, bf16[128,1152]{1,0:T(8,128)(2,1)} %tokens_hbm.1, f32[1152]{0:T(1024)} %shift_hbm.1, f32[1152]{0:T(1024)} %scale_hbm.1, f32[1152]{0:T(1024)} %gate_hbm.1, bf16[1152,3456]{1,0:T(8,128)(2,1)} %w_hbm.1, bf16[1152,1152]{1,0:T(8,128)(2,1)} %wo_hbm.1), custom_call_target="tpu_custom_call" | custom-call | tf_op jit(solution)/shard_map/pallas_call | solution.py:307
  38.5 0.7 %copy.9 = bf16[128,1152]{1,0:T(8,128)(2,1)} copy(bf16[128,1152]{1,0:T(8,128)(2,1)S(1)} %shard_map.73) | data formatting | bytes 589824
